TPU v7x, 256 devices: a whole 4x4x8 slice. The times are simulated.
256 devices in a mesh: occ: 8 (over z), vir: 16 (over y, x), ka: 2 (over core).
Axes of the slice: x: 4, y: 4, z: 8, core: 2. Of those that a mesh axis runs over, the one named last changes fastest.
Arguments:
- lambda_amps: bfloat16 [2, 128, 1024, 1024], P(None, 'occ', 'vir', 'ka'), may hold values from -0.25 to 0.25
- screened_ints: bfloat16 [128, 1024, 1024], P(('occ', 'vir'), 'ka'), may hold values from -6 to 6
- half_ints: bfloat16 [128, 1024, 128], P(('occ', 'vir'), 'ka'), may hold values from -0.5 to 0.5
- singles: bfloat16 [128, 1024], P(None, 'vir'), may hold values from -6 to 6
- block_mask: int32 [128, 8, 8], P('occ', 'ka'), may hold values from 0 to 1, as said below
Outputs:
- residual_part: bfloat16 [2, 128, 1024, 1024], P('ka', 'occ', 'vir')
Inputs may be any that keep to these rules, and one draw needn't show every extreme that they name: `block_mask`: for each j and each of the 2 equal ranges of e blocks, between 1 and 16 of its 32 blocks are 1; some (j, range) has exactly 16.
All inputs are finite; a program needn't handle non-finite values.
Results may differ from a plain program's by a relative error of at most 0.0058.
Values may be sent and summed in bfloat16 or wider, within the bound.
A program may use at most 128 MiB of HBM per device.

v0:
```python
import jax
import jax.numpy as jnp
from jax import lax
from jax.sharding import PartitionSpec as P

TILE = 128


def in_order(pieces, dim):
    pieces = jnp.moveaxis(pieces, 0, dim)
    dims = pieces.shape
    return pieces.reshape(*dims[:dim], dims[dim] * dims[dim + 1], *dims[dim + 2 :])


def copy_for_each(x, axis):
    devices = lax.axis_size(axis)
    return lax.all_to_all(jnp.broadcast_to(x[None], (devices, *x.shape)), axis, 0, 0, tiled=True)


def gather_directly(x, axis, dim):
    return in_order(copy_for_each(x, axis), dim)


def cut_along(x, dim, devices):
    before, after = (x.shape[:dim], x.shape[dim + 1 :])
    return jnp.moveaxis(x.reshape(*before, devices, -1, *after), dim, 0)


def summed_on_arrival(x, axis, dim):
    devices = lax.axis_size(axis)
    pieces = lax.all_to_all(cut_along(x, dim, devices), axis, 0, 0, tiled=True)
    return jnp.sum(pieces.astype(jnp.float32), axis=0)


def edges_of(length, count):
    unit = 8 if length >= 8 * count else 1
    return [length // unit * k // count * unit for k in range(1, count)]


def cut_exchange(x, axis, pieces, split_dim, concat_dim):
    blocks = cut_along(x, split_dim, lax.axis_size(axis))
    cut = max(range(1, max(2, blocks.ndim - 1)), key=lambda d: blocks.shape[d])
    outs = []
    for slab in jnp.split(blocks, edges_of(blocks.shape[cut], pieces), axis=cut):
        if slab.size:
            outs.append(lax.all_to_all(slab, axis, split_axis=0, concat_axis=0, tiled=True))
    return in_order(jnp.concatenate(outs, axis=cut), concat_dim)


def dense_form(screened_ints, half_ints, single_all, own_mask, tile_size):
    per_vir, half_rows, full_cols = screened_ints.shape
    row_blocks = half_rows // tile_size
    col_blocks = full_cols // tile_size
    dressed = screened_ints.astype(jnp.float32) - jnp.einsum(
        "jem,mb->jeb", half_ints, single_all, preferred_element_type=jnp.float32
    )
    block_gate = own_mask.astype(jnp.float32)[:, :, None, :, None]
    screened = dressed.reshape(per_vir, row_blocks, tile_size, col_blocks, tile_size) * block_gate
    return screened.astype(jnp.bfloat16).reshape(per_vir, half_rows, full_cols)


def body(lambda_amps, screened_ints, half_ints, singles, block_mask):
    tile_size = TILE
    single_all = gather_directly(singles, "vir", 1)
    per_vir, half_rows, full_cols = screened_ints.shape
    vir_index = lax.axis_index("vir")
    own_mask = lax.dynamic_slice_in_dim(block_mask, vir_index * per_vir, per_vir, 0)
    local_blocks = dense_form(screened_ints, half_ints, single_all, own_mask, tile_size)
    moved_amps = lax.all_to_all(lambda_amps, "vir", split_axis=1, concat_axis=2, tiled=True)
    summed = summed_on_arrival(
        jnp.einsum(
            "ijae,jeb->ijab", moved_amps, local_blocks, preferred_element_type=jnp.float32
        ).astype(jnp.bfloat16),
        "ka",
        0,
    ).astype(jnp.bfloat16)
    return cut_exchange(summed, "vir", 2, 2, 1)


def solution(mesh):
    return jax.shard_map(
        body,
        mesh=mesh,
        in_specs=(
            P(None, "occ", "vir", "ka"),
            P(("occ", "vir"), "ka", None),
            P(("occ", "vir"), "ka", None),
            P(None, "vir"),
            P("occ", "ka", None),
        ),
        out_specs=P("ka", "occ", "vir", None),
        check_vma=False,
    )
```

profile of v0, /device:TPU:2, one launch (start us, length us, event | category | flops | bytes accessed | tf_op | source)
XLA Modules:
  0.0 112.2 jit_solution(1229316391683924685)
XLA Ops:
  0.0 0.0 copy-start
  0.0 1.8 %copy.16 = bf16[2,16,64,512]{3,2,0,1:T(8,128)(2,1)S(1)} copy(bf16[2,16,64,512]{3,2,1,0:T(8,128)(2,1)} %param.5) | data formatting | bytes 4194304 | tf_op args[0]
  1.9 0.0 copy-start.1
  1.9 0.0 copy-start.2
  1.9 34.4 %all_to_all.29 = bf16[2,16,64,512]{3,2,0,1:T(8,128)(2,1)S(1)} all-to-all(bf16[2,16,64,512]{3,2,0,1:T(8,128)(2,1)S(1)} %copy.16), channel_id=1, replica_groups=mesh['occ'=8,'vir'=16,'ka'=2] {'vir'}, dimensions={1} | all-to-all | bytes 4194304 | tf_op jit(solution)/shard_map/all_to_all | solution.py:69
  36.3 0.0 copy-done.1
  36.3 0.7 broadcast_in_dim.2
  37.0 4.8 %all-to-all-start = ((bf16[16,128,64]{1,2,0:T(8,128)(2,1)}), bf16[16,128,64]{1,2,0:T(8,128)(2,1)S(1)}, u32[]{:S(2)}, u32[]{:S(2)}) async-start(bf16[16,128,64]{1,2,0:T(8,128)(2,1)} %broadcast_in_dim.2), calls=%async_computation | async-start | bytes 524288 | tf_op jit(solution)/shard_map/all_to_all | solution.py:17
  41.8 0.0 copy-done.2
  41.8 0.2 convert_reduce_fusion
  42.0 1.5 %mul.16 = f32[4,128,8,128]{3,2,1,0:T(8,128)} broadcast(f32[4,8]{1,0:T(4,128)S(1)} %convert_reduce_fusion), dimensions={0,2} | broadcast | bytes 2097280 | tf_op jit(solution)/shard_map/mul | solution.py:58
  43.5 2.7 %mul.17 = f32[1,512,1024]{2,1,0:T(8,128)} reshape(f32[4,128,8,128]{3,2,1,0:T(8,128)} %mul.16) | data formatting | bytes 4194304 | tf_op jit(solution)/shard_map/mul | solution.py:58
  46.2 0.0 copy-start.3
  46.2 1.5 %copy.17 = bf16[2,16,64,512]{3,2,1,0:T(8,128)(2,1)} copy(bf16[2,16,64,512]{3,2,0,1:T(8,128)(2,1)S(1)} %all_to_all.29) | data formatting | bytes 4194304 | tf_op jit(solution)/shard_map/all_to_all | solution.py:69
  47.7 1.5 %all-to-all-done = bf16[16,128,64]{1,2,0:T(8,128)(2,1)S(1)} async-done(((bf16[16,128,64]{1,2,0:T(8,128)(2,1)}), bf16[16,128,64]{1,2,0:T(8,128)(2,1)S(1)}, u32[]{:S(2)}, u32[]{:S(2)}) %all-to-all-start) | async-done | bytes 262176 | tf_op jit(solution)/shard_map/all_to_all | solution.py:17
  49.2 0.0 copy-done
  49.2 0.0 copy-done.3
  49.3 6.3 %convert_bitcast_fusion = bf16[2,1,1,1024,1024]{3,4,2,1,0:T(8,128)(2,1)} fusion(bf16[2,1024,512]{2,1,0:T(8,128)(2,1)} %bitcast.46, f32[1,512,1024]{2,1,0:T(8,128)} %mul.17, bf16[128,1024]{0,1:T(8,128)(2,1)S(1)} %bitcast.47, bf16[1,512,1024]{2,1,0:T(8,128)(2,1)S(1)} %copy-done.3, bf16[1,512,128]{2,1,0:T(8,128)(2,1)S(1)} %copy-done), kind=kOutput, calls=%fused_computation.1 | convolution fusion | flops 2285895680 | bytes 9830400 | tf_op jit(solution)/shard_map/ijae,jeb->ijab/dot_general | solution.py:71
  55.6 8.5 %all_to_all.30 = bf16[2,1,1,1024,1024]{3,4,2,1,0:T(8,128)(2,1)S(1)} all-to-all(bf16[2,1,1,1024,1024]{3,4,2,1,0:T(8,128)(2,1)} %convert_bitcast_fusion), channel_id=1, replica_groups=mesh['occ'=8,'vir'=16,'ka'=2] {'ka'}, dimensions={0} | all-to-all | bytes 8388608 | tf_op jit(solution)/shard_map/all_to_all | solution.py:31
  64.1 1.0 bitcast_reduce_fusion
  65.1 2.6 %copy.21 = bf16[1024,1024]{1,0:T(8,128)(2,1)} copy(bf16[1024,1024]{0,1:T(8,128)(2,1)S(1)} %bitcast_reduce_fusion) | data formatting | bytes 4194304 | tf_op jit(solution)/shard_map/reduce_sum | solution.py:32
  67.6 1.7 %slice_bitcast_fusion.1 = (bf16[16,1,1,32,1024]{4,3,2,1,0:T(8,128)(2,1)S(1)}, bf16[16,1,1,32,1024]{4,3,2,1,0:T(8,128)(2,1)S(1)}) fusion(bf16[16,1,1,64,1024]{4,3,0,2,1:T(8,128)(2,1)} %bitcast.45), kind=kLoop, calls=%fused_computation.8 | loop fusion | bytes 4194304 | tf_op jit(solution)/shard_map/split | solution.py:44
  69.4 21.7 %all_to_all.31 = bf16[16,1,1,32,1024]{4,3,2,1,0:T(8,128)(2,1)S(1)} all-to-all(bf16[16,1,1,32,1024]{4,3,2,1,0:T(8,128)(2,1)S(1)} %get-tuple-element.5), channel_id=1, replica_groups=mesh['occ'=8,'vir'=16,'ka'=2] {'vir'}, dimensions={0} | all-to-all | bytes 2097152 | tf_op jit(solution)/shard_map/all_to_all | solution.py:46
  91.1 19.6 %all_to_all.32 = bf16[16,1,1,32,1024]{4,3,2,1,0:T(8,128)(2,1)S(1)} all-to-all(bf16[16,1,1,32,1024]{4,3,2,1,0:T(8,128)(2,1)S(1)} %get-tuple-element.6), channel_id=1, replica_groups=mesh['occ'=8,'vir'=16,'ka'=2] {'vir'}, dimensions={0} | all-to-all | bytes 2097152 | tf_op jit(solution)/shard_map/all_to_all | solution.py:46
  110.7 1.5 %maximum_bitcast_fusion = bf16[1,16,64,1024]{3,2,1,0:T(8,128)(2,1)} fusion(bf16[16,1,1,32,1024]{4,3,2,1,0:T(8,128)(2,1)S(1)} %all_to_all.32, bf16[16,1,1,32,1024]{4,3,2,1,0:T(8,128)(2,1)S(1)} %all_to_all.31), kind=kLoop, calls=%fused_computation.2 | loop fusion | flops 4194304 | bytes 4194304 | tf_op jit(solution)/shard_map/reshape;transpose | solution.py:12
Async XLA Ops:
  0.0 49.2 %copy-start = (bf16[1,512,128]{2,1,0:T(8,128)(2,1)S(1)}, bf16[1,512,128]{2,1,0:T(8,128)(2,1)}, u32[]{:S(2)}) copy-start(bf16[1,512,128]{2,1,0:T(8,128)(2,1)} %param.7) | copy-start | bytes 393220
  1.9 34.5 %copy-start.1 = (bf16[128,64]{0,1:T(8,128)(2,1)S(1)}, bf16[128,64]{0,1:T(8,128)(2,1)}, u32[]{:S(2)}) copy-start(bf16[128,64]{0,1:T(8,128)(2,1)} %param.8) | copy-start | bytes 49156
  1.9 40.0 %copy-start.2 = (s32[16,4,8]{0,2,1:T(8,128)S(1)}, s32[16,4,8]{0,2,1:T(8,128)}, u32[]{:S(2)}) copy-start(s32[16,4,8]{0,2,1:T(8,128)} %param.9) | copy-start | bytes 6148
  37.0 12.2 %all-to-all-start = ((bf16[16,128,64]{1,2,0:T(8,128)(2,1)}), bf16[16,128,64]{1,2,0:T(8,128)(2,1)S(1)}, u32[]{:S(2)}, u32[]{:S(2)}) async-start(bf16[16,128,64]{1,2,0:T(8,128)(2,1)} %broadcast_in_dim.2), calls=%async_computation | async-start | bytes 524288 | tf_op jit(solution)/shard_map/all_to_all | solution.py:17
  46.2 3.0 %copy-start.3 = (bf16[1,512,1024]{2,1,0:T(8,128)(2,1)S(1)}, bf16[1,512,1024]{2,1,0:T(8,128)(2,1)}, u32[]{:S(2)}) copy-start(bf16[1,512,1024]{2,1,0:T(8,128)(2,1)} %param.6) | copy-start | bytes 3145732
where the time goes:
time: 114 us; the launch traced here: 112 us
  blocking collectives  84.2 us (74%)
  local copies, waits for them, and re-layouts  12.6 us (11%)
  matrix products  6.33 us (6%)
  starting transfers between devices  4.78 us (4%)
  other arithmetic  2.69 us (2%)
  waiting for transfers between devices  1.53 us (1%)
    all_to_all x2, blocking collectives, cut_exchange(): lax.all_to_all(slab, axis, split_axis=0, concat_axis=0, tiled=True)  41.3 us
    all_to_all x1, blocking collectives, body(): lax.all_to_all(lambda_amps, 'vir', split_axis=1, concat_axis=2, tiled=True)  34.4 us
    all_to_all x1, blocking collectives, summed_on_arrival(): pieces = lax.all_to_all(cut_along(x, dim, devices), axis, 0, 0, tiled=True)  8.48 us
    dot_general x1, matrix products, body(): jnp.einsum('ijae,jeb->ijab', moved_amps, local_blocks, preferred_element_...  6.33 us
    all_to_all x1, starting transfers between devices, copy_for_each(): lax.all_to_all(jnp.broadcast_to(x[None], (devices, *x.shape)), axis, 0, 0...  4.78 us
    mul x2, local copies, waits for them, and re-layouts, dense_form(): dressed.reshape(per_vir, row_blocks, tile_size, col_blocks, tile_size)  4.23 us
    reduce_sum x1, local copies, waits for them, and re-layouts, summed_on_arrival(): return jnp.sum(pieces.astype(jnp.float32), axis=0)  2.56 us
  transfers between devices with their start and end apart: 1, of which 1 were waited for; matrix products, arithmetic and copies ran while one was open for 5% of the time, Pallas kernels for 0%

commit v1 on v0

v1 whole, which is shorter than its diff:
```python
import functools

import jax
import jax.numpy as jnp
from jax import lax
from jax.experimental import pallas as pl
from jax.experimental.pallas import tpu as pltpu
from jax.sharding import PartitionSpec as P

MESH = pl.DeviceIdType.MESH
TILE = 128
CAP = 16
CHUNK = 4
SIDE = 4
SIGNS = (-1, 1, 1, -1)
STEPS = ((0, 0), (1, 0), (0, 1), (1, 1))


def wrap(k):
    return lax.rem(k + 2 * SIDE, SIDE)


def sign_of(k):
    return 1 - 2 * lax.rem(k, 2)


def place(x, y):
    return wrap(y) * SIDE + wrap(x)


def owner_of(x, y, q):
    sx, sy = sign_of(y), sign_of(x)
    return (place(x, y), place(x - sx, y), place(x, y - sy), place(x + sx, y + sy))[q]


def kernel(
    amps, ints, half, singles, mask, out,
    lbuf, bbuf0, bbuf1, bbuf2, bbuf3, xbuf, ybuf, tbuf, give, take, acc, done, slot, nxt,
    lsend, lrecv, lown, inload, tsend, trecv, dsend, drecv, bsend, brecv, rsend, rrecv,
    psend, precv, osend, orecv, oown,
):
    bbuf = (bbuf0, bbuf1, bbuf2, bbuf3)
    vir = lax.axis_index("vir")
    ka = lax.axis_index("ka")
    other = 1 - ka
    x, y = lax.rem(vir, SIDE), vir // SIDE
    sx, sy = sign_of(y), sign_of(x)
    peers = SIDE * SIDE

    loads = [
        pltpu.make_async_copy(
            singles.at[pl.ds(ka * 32, 32)], tbuf.at[vir // 2, lax.rem(vir, 2), ka], inload.at[0]
        ),
    ]
    loads += [
        pltpu.make_async_copy(half.at[0, pl.ds(e * TILE, TILE)], ybuf.at[e], inload.at[1 + e])
        for e in range(4)
    ]
    loads += [
        pltpu.make_async_copy(
            ints.at[0, pl.ds(e * TILE, TILE), pl.ds(b * TILE, TILE)],
            xbuf.at[b, e],
            inload.at[5 + 4 * b + e],
        )
        for b in range(8)
        for e in range(4)
    ]
    for copy in loads:
        copy.start()
    own_loads = []
    for q in range(4):
        j = owner_of(x, y, q)
        own_loads.append(pltpu.make_async_copy(amps.at[:, j], lbuf.at[q, :, 0], lown.at[q]))
    for copy in own_loads:
        copy.start()

    barrier = pltpu.get_barrier_semaphore()

    def greet(r, carry):
        pl.semaphore_signal(
            barrier, inc=1, device_id={"vir": lax.rem(vir + r, peers)}, device_id_type=MESH
        )
        return carry

    lax.fori_loop(1, peers, greet, 0)
    pl.semaphore_signal(barrier, inc=1, device_id={"ka": other}, device_id_type=MESH)

    pl.semaphore_wait(barrier, peers)

    def t_copy(r):
        return pltpu.make_async_remote_copy(
            src_ref=singles.at[pl.ds(ka * 32, 32)],
            dst_ref=tbuf.at[vir // 2, lax.rem(vir, 2), ka],
            send_sem=tsend.at[r - 1],
            recv_sem=trecv.at[r - 1],
            device_id={"vir": lax.rem(vir + r, peers)},
            device_id_type=MESH,
        )

    def t_start(r, carry):
        t_copy(r).start()
        return carry

    lax.fori_loop(1, peers, t_start, 0)

    def l_copy(q, d):
        dx, dy = STEPS[d]
        hx = wrap(x - dx * SIGNS[q] * sx * (1 - 2 * dy))
        hy = wrap(y - dy * SIGNS[q] * sy * (1 - 2 * dx))
        return pltpu.make_async_remote_copy(
            src_ref=amps.at[:, owner_of(hx, hy, q)],
            dst_ref=lbuf.at[q, :, d],
            send_sem=lsend.at[q, d - 1],
            recv_sem=lrecv.at[q, d - 1],
            device_id={"vir": place(hx, hy)},
            device_id_type=MESH,
        )

    l_copies = [[l_copy(q, d) for d in (1, 2, 3)] for q in range(4)]
    for q in range(4):
        for copy in l_copies[q]:
            copy.start()

    for q in range(4):
        j = owner_of(x, y, q)

        def count(p, c, q=q, j=j):
            live = mask[lax.shift_right_logical(p, 3), lax.bitwise_and(p, 7), j]
            slot[q, p] = live * c + (1 - live) * CAP
            return c + live

        lax.fori_loop(0, 32, count, 0)

    nxt[32] = 31

    def search(k, c):
        p = 31 - k
        live = mask[lax.shift_right_logical(p, 3), lax.bitwise_and(p, 7), vir]
        c = live * p + (1 - live) * c
        nxt[p] = c
        return c

    lax.fori_loop(0, 32, search, 31)

    for q in range(4):
        bbuf[q][CAP] = jnp.zeros((TILE, TILE), jnp.bfloat16)

    def t_wait(r, carry):
        t_copy(r).wait_recv()
        return carry

    lax.fori_loop(1, peers, t_wait, 0)
    loads[0].wait()
    d_copy = pltpu.make_async_remote_copy(
        src_ref=tbuf.at[:, :, ka],
        dst_ref=tbuf.at[:, :, ka],
        send_sem=dsend,
        recv_sem=drecv,
        device_id={"ka": other},
        device_id_type=MESH,
    )
    d_copy.start()
    d_copy.wait_recv()
    for copy in loads[1:]:
        copy.wait()

    def b_copy(axis, c):
        return pltpu.make_async_remote_copy(
            src_ref=bbuf[0].at[pl.ds(c * CHUNK, CHUNK)],
            dst_ref=bbuf[1 + axis].at[pl.ds(c * CHUNK, CHUNK)],
            send_sem=bsend.at[axis, c],
            recv_sem=brecv.at[axis, c],
            device_id={"vir": place(x, y + sy) if axis else place(x + sx, y)},
            device_id_type=MESH,
        )

    def relay_copy(axis, k):
        c = 2 * axis + k
        return pltpu.make_async_remote_copy(
            src_ref=bbuf[1 + axis].at[pl.ds(c * CHUNK, CHUNK)],
            dst_ref=bbuf[3].at[pl.ds(c * CHUNK, CHUNK)],
            send_sem=rsend.at[axis, k],
            recv_sem=rrecv.at[axis, k],
            device_id={"vir": place(x - sx, y) if axis else place(x, y - sy)},
            device_id_type=MESH,
        )

    b_copies = [[b_copy(axis, c) for c in range(4)] for axis in range(2)]
    relays = [[relay_copy(axis, k) for k in range(2)] for axis in range(2)]

    def dress(k, p):
        p = nxt[p]
        e = lax.shift_right_logical(p, 3)
        b = lax.bitwise_and(p, 7)
        inner = lax.dot_general(
            ybuf[e],
            tbuf[b].reshape(TILE, TILE),
            (((1,), (1,)), ((), ())),
            preferred_element_type=jnp.float32,
        )
        value = xbuf[b, e].astype(jnp.float32) - inner
        bbuf[0][k] = value.astype(jnp.bfloat16)
        return p + 1

    p = lax.fori_loop(0, 8, dress, 0)
    b_copies[0][0].start()
    p = lax.fori_loop(8, 12, dress, p)
    b_copies[0][1].start()
    p = lax.fori_loop(12, 16, dress, p)
    b_copies[1][2].start()
    b_copies[0][2].start()
    b_copies[1][3].start()
    b_copies[0][3].start()
    b_copies[1][0].start()
    b_copies[1][1].start()

    def give_copy(q):
        return pltpu.make_async_remote_copy(
            src_ref=give.at[q],
            dst_ref=take.at[q],
            send_sem=psend.at[q],
            recv_sem=precv.at[q],
            device_id={"ka": other},
            device_id_type=MESH,
        )

    def out_copy(q, d):
        dx, dy = STEPS[d]
        return pltpu.make_async_remote_copy(
            src_ref=done.at[q, d],
            dst_ref=out.at[0, owner_of(x, y, q)],
            send_sem=osend.at[q, d - 1],
            recv_sem=orecv.at[q, d - 1],
            device_id={"vir": place(x + dx * SIGNS[q] * sx, y + dy * SIGNS[q] * sy)},
            device_id_type=MESH,
        )

    def in_copy(q, d):
        dx, dy = STEPS[d]
        hx = wrap(x - dx * SIGNS[q] * sx * (1 - 2 * dy))
        hy = wrap(y - dy * SIGNS[q] * sy * (1 - 2 * dx))
        return pltpu.make_async_remote_copy(
            src_ref=done.at[q, d],
            dst_ref=out.at[0, owner_of(hx, hy, q)],
            send_sem=osend.at[q, d - 1],
            recv_sem=orecv.at[q, d - 1],
            device_id={"vir": place(hx, hy)},
            device_id_type=MESH,
        )

    gives = [give_copy(q) for q in range(4)]
    outs = [[out_copy(q, d) for d in (1, 2, 3)] for q in range(4)]
    own_outs = [
        pltpu.make_async_copy(done.at[q, 0], out.at[0, owner_of(x, y, q)], oown.at[q])
        for q in range(4)
    ]

    def multiply(q):
        own_loads[q].wait()
        for copy in l_copies[q]:
            copy.wait_recv()

        def columns(n, carry):
            pieces = []
            for e in range(4):
                pieces.append(
                    jnp.concatenate(
                        [bbuf[q][slot[q, 8 * e + 2 * n + k]] for k in range(2)], axis=1
                    )
                )
            rhs = jnp.concatenate(pieces, axis=0)
            where = pl.ds(pl.multiple_of(n * 2 * TILE, 2 * TILE), 2 * TILE)
            lhs = lbuf[q, other].reshape(256, 512)
            part = jnp.dot(lhs, rhs, preferred_element_type=jnp.float32)
            give[q, :, :, where] = part.astype(jnp.bfloat16).reshape(4, 64, 2 * TILE)
            lhs = lbuf[q, ka].reshape(256, 512)
            part = jnp.dot(lhs, rhs, preferred_element_type=jnp.float32)
            acc[q, :, :, where] = part.reshape(4, 64, 2 * TILE)
            return carry

        lax.fori_loop(0, 4, columns, 0)
        gives[q].start()

    def finish(q):
        gives[q].wait_recv()
        for d in (3, 1, 2, 0):
            total = acc[q, d] + take[q, d].astype(jnp.float32)
            done[q, d] = total.astype(jnp.bfloat16)
        for d in (3, 1, 2):
            outs[q][d - 1].start()
        own_outs[q].start()

    multiply(0)
    b_copies[0][0].wait_recv()
    relays[0][0].start()
    b_copies[1][2].wait_recv()
    relays[1][0].start()
    b_copies[0][1].wait_recv()
    relays[0][1].start()
    b_copies[1][3].wait_recv()
    relays[1][1].start()
    finish(0)
    b_copies[0][2].wait_recv()
    b_copies[0][3].wait_recv()
    multiply(1)
    b_copies[1][0].wait_recv()
    b_copies[1][1].wait_recv()
    multiply(2)
    finish(1)
    for axis in range(2):
        for k in range(2):
            relays[axis][k].wait_recv()
    multiply(3)
    finish(2)
    finish(3)

    def t_sent(r, carry):
        t_copy(r).wait_send()
        return carry

    lax.fori_loop(1, peers, t_sent, 0)
    d_copy.wait_send()
    for q in range(4):
        gives[q].wait_send()
        own_outs[q].wait()
        for d in (1, 2, 3):
            l_copies[q][d - 1].wait_send()
            outs[q][d - 1].wait_send()
            in_copy(q, d).wait_recv()
    for axis in range(2):
        for c in range(4):
            b_copies[axis][c].wait_send()
        for k in range(2):
            relays[axis][k].wait_send()


def body(lambda_amps, screened_ints, half_ints, singles, block_mask):
    bf16, f32 = jnp.bfloat16, jnp.float32
    dma = pltpu.SemaphoreType.DMA
    anywhere = pl.BlockSpec(memory_space=pl.ANY)
    return pl.pallas_call(
        kernel,
        out_shape=jax.ShapeDtypeStruct((1, 16, 64, 1024), bf16),
        in_specs=[anywhere] * 4 + [pl.BlockSpec(memory_space=pltpu.SMEM)],
        out_specs=anywhere,
        scratch_shapes=[
            pltpu.VMEM((4, 2, 4, 64, 512), bf16),
            pltpu.VMEM((CAP + 1, TILE, TILE), bf16),
            pltpu.VMEM((CAP + 1, TILE, TILE), bf16),
            pltpu.VMEM((CAP + 1, TILE, TILE), bf16),
            pltpu.VMEM((CAP + 1, TILE, TILE), bf16),
            pltpu.VMEM((8, 4, TILE, TILE), bf16),
            pltpu.VMEM((4, TILE, TILE), bf16),
            pltpu.VMEM((8, 2, 2, 32, TILE), bf16),
            pltpu.VMEM((4, 4, 64, 1024), bf16),
            pltpu.VMEM((4, 4, 64, 1024), bf16),
            pltpu.VMEM((4, 4, 64, 1024), f32),
            pltpu.VMEM((4, 4, 64, 1024), bf16),
            pltpu.SMEM((4, 32), jnp.int32),
            pltpu.SMEM((40,), jnp.int32),
            dma((4, 3)), dma((4, 3)), dma((4,)), dma((37,)),
            dma((15,)), dma((15,)), dma, dma,
            dma((2, 4)), dma((2, 4)), dma((2, 2)), dma((2, 2)),
            dma((4,)), dma((4,)), dma((4, 3)), dma((4, 3)), dma((4,)),
        ],
        compiler_params=pltpu.CompilerParams(collective_id=0, has_side_effects=True),
        cost_estimate=pl.CostEstimate(
            flops=2 * 2048 * 512 * 1024, bytes_accessed=6 << 20, transcendentals=0
        ),
    )(lambda_amps, screened_ints, half_ints, singles.T, jnp.transpose(block_mask, (1, 2, 0)))


def solution(mesh):
    return jax.shard_map(
        body,
        mesh=mesh,
        in_specs=(
            P(None, "occ", "vir", "ka"),
            P(("occ", "vir"), "ka", None),
            P(("occ", "vir"), "ka", None),
            P(None, "vir"),
            P("occ", "ka", None),
        ),
        out_specs=P("ka", "occ", "vir", None),
        check_vma=False,
    )
```

time: 114 us -> 53.5 us (0.47); the launches traced: 112 us -> 53.1 us
  blocking collectives: 84.2 us -> 0 us
  Pallas kernels: 0 us -> 49.9 us
  local copies, waits for them, and re-layouts: 12.6 us -> 3.14 us
  matrix products: 6.33 us -> 0 us
  starting transfers between devices: 4.78 us -> 0 us
  other arithmetic: 2.69 us -> 0 us
  waiting for transfers between devices: 1.53 us -> 0 us
    all_to_all x4 -> x0, blocking collectives: 84.2 us -> none  [the longest x2 41.3 us: cut_exchange(): lax.all_to_all(slab, axis, split_axis=0, concat_axis=0, tiled=True)]
    pallas_call x0 -> x1, Pallas kernels: none -> 49.9 us  [body(): pl.pallas_call(kernel, out_shape=jax.ShapeDtypeStruct((1, 16, 64, 1024),...]
    dot_general x1 -> x0, matrix products: 6.33 us -> none  [body(): jnp.einsum('ijae,jeb->ijab', moved_amps, local_blocks, preferred_element_...]
    all_to_all x1 -> x0, starting transfers between devices: 4.78 us -> none  [copy_for_each(): lax.all_to_all(jnp.broadcast_to(x[None], (devices, *x.shape)), axis, 0, 0...]
    mul x2 -> x0, local copies, waits for them, and re-layouts: 4.23 us -> none  [dense_form(): dressed.reshape(per_vir, row_blocks, tile_size, col_blocks, tile_size)]
    reduce_sum x1 -> x0, local copies, waits for them, and re-layouts: 2.56 us -> none  [summed_on_arrival(): return jnp.sum(pieces.astype(jnp.float32), axis=0)]
    split x1 -> x0, local copies, waits for them, and re-layouts: 1.71 us -> none  [cut_exchange(): jnp.split(blocks, edges_of(blocks.shape[cut], pieces), axis=cut)]
    all_to_all x1 -> x0, waiting for transfers between devices: 1.53 us -> none  [copy_for_each(): lax.all_to_all(jnp.broadcast_to(x[None], (devices, *x.shape)), axis, 0, 0...]
  transfers between devices with their start and end apart: 1 -> 0, of which waited for: 1 -> 0; matrix products, arithmetic and copies ran while one was open for 5% -> 0% of each run, Pallas kernels for 0% -> 0%
where the time goes in v1:
time: 53.5 us; the launch traced here: 53.1 us
  Pallas kernels  49.9 us (93%)
  local copies, waits for them, and re-layouts  3.14 us (6%)
    pallas_call x1, Pallas kernels, body(): pl.pallas_call(kernel, out_shape=jax.ShapeDtypeStruct((1, 16, 64, 1024),...  49.9 us
    unnamed x1, local copies, waits for them, and re-layouts  3.14 us

profile of v1, /device:TPU:2, one launch (start us, length us, event | category | flops | bytes accessed | tf_op | source)
XLA Modules:
  0.0 53.1 jit_solution(3408717412608750993)
XLA Ops:
  0.0 49.9 %shard_map.55 = bf16[1,16,64,1024]{3,2,1,0:T(8,128)(2,1)} custom-call(bf16[2,16,64,512]{3,2,1,0:T(8,128)(2,1)} %amps.1, bf16[1,512,1024]{2,1,0:T(8,128)(2,1)} %ints.1, bf16[1,512,128]{2,1,0:T(8,128)(2,1)} %half.1, bf16[64,128]{1,0:T(8,128)(2,1)} %bitcast.2, s32[4,8,16]{2,1,0:T(8,128)} %bitcast.3), custom_call_target="tpu_custom_call" | custom-call | flops 2147483648 | bytes 6291456 | tf_op jit(solution)/shard_map/pallas_call | solution.py:341
  49.9 3.1 %copy.7 = bf16[1,16,64,1024]{3,2,1,0:T(8,128)(2,1)} copy(bf16[1,16,64,1024]{3,2,1,0:T(8,128)(2,1)} %shard_map.55) | data formatting | bytes 4194304

commit v2 on v0

v2 whole, which is shorter than its diff:
```python
import jax
import jax.numpy as jnp
from jax import lax
from jax.experimental import pallas as pl
from jax.experimental.pallas import tpu as pltpu
from jax.sharding import PartitionSpec as P

MESH = pl.DeviceIdType.MESH
TILE = 128
CHUNK = 5
EMPTY = 20
SIDE = 4
HOLD = ((0, 0), (1, 0), (0, 1), (1, 1))
AROUND = tuple((a, b) for a in (-1, 0, 1) for b in (-1, 0, 1) if (a, b) != (0, 0))
EDGES = (
    (0, 1, (1, 0), (0, 2, 3)),
    (0, 2, (0, 1), (1, 2, 3)),
    (1, 3, (0, 1), (0, 2)),
    (2, 3, (1, 0), (1, 3)),
    (3, 2, (-1, 0), (0,)),
    (3, 1, (0, -1), (1,)),
)
START = (
    (1, 1, 0), (1, 2, 1), (0, 0, 1), (0, 0, 2), (1, 1, 2), (1, 2, 2), (0, 1, 1), (0, 2, 2),
    (1, 1, 3), (1, 2, 3),
)
MIDDLE = ((0, 3), (1, 3), (2, 3), (1, 2), (2, 1))
LATE = ((3, 3), (3, 1), (3, 2))
RELAYS = (
    ((1, -1), (-1, 0)), ((1, 0), (-1, 0)), ((1, 1), (-1, 0)),
    ((-1, 1), (0, -1)), ((0, 1), (0, -1)), ((1, 1), (0, -1)),
    ((1, 1), (-1, -1)),
)


def served(q):
    ax, ay = HOLD[q]
    ux, uy = 2 * ax - 1, 2 * ay - 1
    return ((0, 0), (ux, 0), (0, uy), (ux, uy))


def parity(a, b):
    return 1 - 2 * ((a + b) % 2)


def wrap(k):
    return lax.rem(k + 2 * SIDE, SIDE)


def place(x, y):
    return wrap(y) * SIDE + wrap(x)


def kernel(
    amps, ints, half, singles, mask_in, out,
    lbuf, bbuf0, bbuf1, bbuf2, bbuf3, xbuf, tbuf, give, take, acc, done,
    mask, slot, nxt,
    lsend, lrecv, lown, inload, tsend, trecv, rsend, rrecv, dsend, drecv, bsend, brecv,
    psend, precv, osend, orecv,
):
    bbuf = (bbuf0, bbuf1, bbuf2, bbuf3)
    vir = lax.axis_index("vir")
    ka = lax.axis_index("ka")
    other = 1 - ka
    x, y = lax.rem(vir, SIDE), vir // SIDE
    sign = 1 - 2 * lax.rem(x + y, 2)

    def near(a, b):
        return place(x + a, y + b)

    def block(v):
        return tbuf.at[v // 2, lax.rem(v, 2), ka]

    def held(q):
        ax, ay = HOLD[q]
        s = sign * parity(ax, ay)
        return near(-s * ax, -s * ay)

    def remote(src, dst, send, recv, v):
        return pltpu.make_async_remote_copy(
            src_ref=src, dst_ref=dst, send_sem=send, recv_sem=recv,
            device_id={"vir": v}, device_id_type=MESH,
        )

    def partner(src, dst, send, recv):
        return pltpu.make_async_remote_copy(
            src_ref=src, dst_ref=dst, send_sem=send, recv_sem=recv,
            device_id={"ka": other}, device_id_type=MESH,
        )

    barrier = pltpu.get_barrier_semaphore()
    for a, b in AROUND:
        pl.semaphore_signal(
            barrier, inc=1, device_id={"vir": near(a, b)}, device_id_type=MESH
        )
    pl.semaphore_signal(barrier, inc=1, device_id={"ka": other}, device_id_type=MESH)

    own_t = pltpu.make_async_copy(singles.at[pl.ds(ka * 32, 32)], block(vir), inload.at[0])
    own_t.start()
    mask_load = pltpu.make_async_copy(mask_in, mask, inload.at[1])
    mask_load.start()
    loads = [
        pltpu.make_async_copy(half.at[0, pl.ds(e * TILE, TILE)], bbuf0.at[CHUNK * e + 4], inload.at[2 + e])
        for e in range(4)
    ]
    loads += [
        pltpu.make_async_copy(
            ints.at[0, pl.ds(e * TILE, TILE), pl.ds(b * TILE, TILE)],
            xbuf.at[b, e],
            inload.at[6 + 4 * b + e],
        )
        for b in range(8)
        for e in range(4)
    ]
    loads += [
        pltpu.make_async_copy(amps.at[:, held(q)], lbuf.at[q, :, 0], lown.at[q])
        for q in range(4)
    ]
    for copy in loads:
        copy.start()
    own_l = loads[-4:]
    loads = loads[:-4]

    t_first = [
        remote(block(vir), block(vir), tsend.at[k], trecv.at[k], near(a, b))
        for k, (a, b) in enumerate(AROUND)
    ]
    t_from = [
        remote(block(near(-a, -b)), block(near(-a, -b)), tsend.at[k], trecv.at[k], near(a, b))
        for k, (a, b) in enumerate(AROUND)
    ]
    t_second = [
        remote(block(near(*what)), block(near(*what)), rsend.at[k], rrecv.at[k], near(*to))
        for k, (what, to) in enumerate(RELAYS)
    ]
    t_second_from = [
        remote(
            block(near(what[0] - to[0], what[1] - to[1])),
            block(near(what[0] - to[0], what[1] - to[1])),
            rsend.at[k], rrecv.at[k], near(*to),
        )
        for k, (what, to) in enumerate(RELAYS)
    ]

    def holder(q, d):
        ax, ay = HOLD[q]
        dx, dy = served(q)[d]
        s = sign * parity(ax + dx, ay + dy)
        return near(-s * dx, -s * dy), near(-s * (ax + dx), -s * (ay + dy))

    l_copies, ins = {}, {}
    for q in range(4):
        for d in (1, 2, 3):
            h, j = holder(q, d)
            l_copies[q, d] = remote(
                amps.at[:, j], lbuf.at[q, :, d], lsend.at[q, d - 1], lrecv.at[q, d - 1], h
            )
            ins[q, d] = remote(
                done.at[q, d - 1], out.at[0, j], osend.at[q, d - 1], orecv.at[q, d - 1], h
            )

    b_copies = {}
    for p, q, (dx, dy), chunks in EDGES:
        s = sign * parity(*HOLD[p])
        for c in chunks:
            piece = pl.ds(c * CHUNK, CHUNK)
            b_copies[q, c] = remote(
                bbuf[p].at[piece], bbuf[q].at[piece],
                bsend.at[q - 1, c], brecv.at[q - 1, c], near(s * dx, s * dy),
            )

    gives = [partner(give.at[q], take.at[q], psend.at[q], precv.at[q]) for q in range(4)]

    outs = {}
    for q in range(4):
        s = sign * parity(*HOLD[q])
        for d in (1, 2, 3):
            dx, dy = served(q)[d]
            outs[q, d] = remote(
                done.at[q, d - 1], out.at[0, held(q)],
                osend.at[q, d - 1], orecv.at[q, d - 1], near(s * dx, s * dy),
            )

    mask_load.wait()
    for q in range(4):
        j = held(q)

        def count(p, c, q=q, j=j):
            live = mask[lax.shift_right_logical(p, 3), lax.bitwise_and(p, 7), j]
            slot[q, p] = live * (c + lax.shift_right_logical(c, 2)) + (1 - live) * EMPTY
            return c + live

        lax.fori_loop(0, 32, count, 0)
        bbuf[q][EMPTY] = jnp.zeros((TILE, TILE), jnp.bfloat16)

    nxt[32] = 31

    def search(k, c):
        p = 31 - k
        live = mask[lax.shift_right_logical(p, 3), lax.bitwise_and(p, 7), vir]
        c = live * p + (1 - live) * c
        nxt[p] = c
        return c

    lax.fori_loop(0, 32, search, 31)

    for copy in loads:
        copy.wait()

    def pack(k, p):
        p = nxt[p]
        bbuf0[k + lax.shift_right_logical(k, 2)] = xbuf[
            lax.bitwise_and(p, 7), lax.shift_right_logical(p, 3)
        ]
        return p + 1

    lax.fori_loop(0, 16, pack, 0)

    own_t.wait()
    pl.semaphore_wait(barrier, 9)

    for copy in t_first:
        copy.start()
    for kind, one, two in START:
        (b_copies if kind else l_copies)[one, two].start()
    for copy in t_from:
        copy.wait_recv()
    for copy in t_second:
        copy.start()

    def multiply(q):
        own_l[q].wait()
        for d in (1, 2, 3):
            l_copies[q, d].wait_recv()
        j = held(q)

        def columns(n, carry):
            amount = jnp.concatenate([bbuf[q][CHUNK * e + 4] for e in range(4)], axis=0)
            inner = lax.dot_general(
                amount,
                tbuf[pl.ds(2 * n, 2)].reshape(2 * TILE, TILE),
                (((1,), (1,)), ((), ())),
                preferred_element_type=jnp.float32,
            )
            pieces = []
            for e in range(4):
                row = []
                for k in range(2):
                    gate = mask[e, 2 * n + k, j].astype(jnp.float32)
                    value = bbuf[q][slot[q, 8 * e + 2 * n + k]].astype(jnp.float32)
                    value -= inner[e * TILE : (e + 1) * TILE, k * TILE : (k + 1) * TILE]
                    row.append((gate * value).astype(jnp.bfloat16))
                pieces.append(jnp.concatenate(row, axis=1))
            rhs = jnp.concatenate(pieces, axis=0)
            where = pl.ds(pl.multiple_of(n * 2 * TILE, 2 * TILE), 2 * TILE)
            lhs = lbuf[q, other].reshape(256, 512)
            part = jnp.dot(lhs, rhs, preferred_element_type=jnp.float32)
            give[q, :, :, where] = part.astype(jnp.bfloat16).reshape(4, 64, 2 * TILE)
            lhs = lbuf[q, ka].reshape(256, 512)
            part = jnp.dot(lhs, rhs, preferred_element_type=jnp.float32)
            acc[q, :, :, where] = part.reshape(4, 64, 2 * TILE)
            return carry

        lax.fori_loop(0, 4, columns, 0)
        gives[q].start()

    def finish(q, ds):
        for d in ds:
            total = acc[q, d] + take[q, d].astype(jnp.float32)
            if d:
                done[q, d - 1] = total.astype(jnp.bfloat16)
            else:
                out[0, held(q)] = total.astype(jnp.bfloat16)

    def send(*which):
        for q, d in which:
            outs[q, d].start()

    def relay(q, c, r):
        b_copies[q, c].wait_recv()
        b_copies[r, c].start()

    relay(1, 0, 3)
    relay(2, 1, 3)
    for q, d in MIDDLE:
        l_copies[q, d].start()
    relay(1, 2, 3)
    relay(3, 0, 2)
    relay(3, 1, 1)
    relay(2, 3, 3)
    for q, d in LATE:
        l_copies[q, d].start()

    for copy in t_second_from:
        copy.wait_recv()
    t_half = partner(tbuf.at[:, :, ka], tbuf.at[:, :, ka], dsend, drecv)
    t_half.start()
    partner(tbuf.at[:, :, other], tbuf.at[:, :, other], dsend, drecv).wait_recv()

    multiply(0)
    gives[0].wait_recv()
    finish(0, (0, 1, 2, 3))
    send((0, 3), (0, 1), (0, 2))
    for c in (1, 3):
        b_copies[1, c].wait_recv()
    multiply(1)
    for c in (0, 2):
        b_copies[2, c].wait_recv()
    multiply(2)
    gives[1].wait_recv()
    finish(1, (3, 1, 2, 0))
    gives[2].wait_recv()
    finish(2, (3, 1, 2, 0))
    send((1, 3), (2, 3), (1, 1), (2, 1), (1, 2), (2, 2))
    for c in (2, 3):
        b_copies[3, c].wait_recv()
    multiply(3)
    gives[3].wait_recv()
    finish(3, (3, 1, 2, 0))
    send((3, 3), (3, 1), (3, 2))

    for copy in t_first + t_second + [t_half] + gives:
        copy.wait_send()
    for copies in (l_copies, b_copies, outs):
        for copy in copies.values():
            copy.wait_send()
    for copy in ins.values():
        copy.wait_recv()


def body(lambda_amps, screened_ints, half_ints, singles, block_mask):
    bf16, f32 = jnp.bfloat16, jnp.float32
    dma = pltpu.SemaphoreType.DMA
    anywhere = pl.BlockSpec(memory_space=pl.ANY)
    return pl.pallas_call(
        kernel,
        out_shape=pltpu.VMEM((1, 16, 64, 1024), bf16),
        in_specs=[anywhere] * 5,
        out_specs=pl.BlockSpec(memory_space=pltpu.VMEM),
        scratch_shapes=[
            pltpu.VMEM((4, 2, 4, 64, 512), bf16),
            pltpu.VMEM((EMPTY + 1, TILE, TILE), bf16),
            pltpu.VMEM((EMPTY + 1, TILE, TILE), bf16),
            pltpu.VMEM((EMPTY + 1, TILE, TILE), bf16),
            pltpu.VMEM((EMPTY + 1, TILE, TILE), bf16),
            pltpu.VMEM((8, 4, TILE, TILE), bf16),
            pltpu.VMEM((8, 2, 2, 32, TILE), bf16),
            pltpu.VMEM((4, 4, 64, 1024), bf16),
            pltpu.VMEM((4, 4, 64, 1024), bf16),
            pltpu.VMEM((4, 4, 64, 1024), f32),
            pltpu.VMEM((4, 3, 64, 1024), bf16),
            pltpu.SMEM((4, 8, 16), jnp.int32),
            pltpu.SMEM((4, 32), jnp.int32),
            pltpu.SMEM((40,), jnp.int32),
            dma((4, 3)), dma((4, 3)), dma((4,)), dma((38,)),
            dma((8,)), dma((8,)), dma((7,)), dma((7,)), dma, dma,
            dma((3, 4)), dma((3, 4)),
            dma((4,)), dma((4,)), dma((4, 3)), dma((4, 3)),
        ],
        compiler_params=pltpu.CompilerParams(collective_id=0, has_side_effects=True),
        cost_estimate=pl.CostEstimate(
            flops=2 * 2048 * 512 * 1024, bytes_accessed=6 << 20, transcendentals=0
        ),
    )(
        lambda_amps, screened_ints, half_ints, singles.T,
        jnp.transpose(block_mask, (1, 2, 0)),
    )


def solution(mesh):
    return jax.shard_map(
        body,
        mesh=mesh,
        in_specs=(
            P(None, "occ", "vir", "ka"),
            P(("occ", "vir"), "ka", None),
            P(("occ", "vir"), "ka", None),
            P(None, "vir"),
            P("occ", "ka", None),
        ),
        out_specs=P("ka", "occ", "vir", None),
        check_vma=False,
    )
```

time: 114 us -> 51.7 us (0.45); the launches traced: 112 us -> 51.1 us
  blocking collectives: 84.2 us -> 0 us
  Pallas kernels: 0 us -> 49.7 us
  local copies, waits for them, and re-layouts: 12.6 us -> 1.32 us
  matrix products: 6.33 us -> 0 us
  starting transfers between devices: 4.78 us -> 0 us
  other arithmetic: 2.69 us -> 0 us
  waiting for transfers between devices: 1.53 us -> 0 us
    all_to_all x4 -> x0, blocking collectives: 84.2 us -> none  [the longest x2 41.3 us: cut_exchange(): lax.all_to_all(slab, axis, split_axis=0, concat_axis=0, tiled=True)]
    pallas_call x0 -> x1, Pallas kernels: none -> 49.7 us  [body(): pl.pallas_call(kernel, out_shape=pltpu.VMEM((1, 16, 64, 1024), bf16), in_...]
    dot_general x1 -> x0, matrix products: 6.33 us -> none  [body(): jnp.einsum('ijae,jeb->ijab', moved_amps, local_blocks, preferred_element_...]
    all_to_all x1 -> x0, starting transfers between devices: 4.78 us -> none  [copy_for_each(): lax.all_to_all(jnp.broadcast_to(x[None], (devices, *x.shape)), axis, 0, 0...]
    mul x2 -> x0, local copies, waits for them, and re-layouts: 4.23 us -> none  [dense_form(): dressed.reshape(per_vir, row_blocks, tile_size, col_blocks, tile_size)]
    reduce_sum x1 -> x0, local copies, waits for them, and re-layouts: 2.56 us -> none  [summed_on_arrival(): return jnp.sum(pieces.astype(jnp.float32), axis=0)]
    split x1 -> x0, local copies, waits for them, and re-layouts: 1.71 us -> none  [cut_exchange(): jnp.split(blocks, edges_of(blocks.shape[cut], pieces), axis=cut)]
    all_to_all x1 -> x0, waiting for transfers between devices: 1.53 us -> none  [copy_for_each(): lax.all_to_all(jnp.broadcast_to(x[None], (devices, *x.shape)), axis, 0, 0...]
  transfers between devices with their start and end apart: 1 -> 0, of which waited for: 1 -> 0; matrix products, arithmetic and copies ran while one was open for 5% -> 0% of each run, Pallas kernels for 0% -> 0%
where the time goes in v2:
time: 51.7 us; the launch traced here: 51.1 us
  Pallas kernels  49.7 us (96%)
  local copies, waits for them, and re-layouts  1.32 us (3%)
    pallas_call x1, Pallas kernels, body(): pl.pallas_call(kernel, out_shape=pltpu.VMEM((1, 16, 64, 1024), bf16), in_...  49.7 us
    unnamed x1, local copies, waits for them, and re-layouts  1.32 us

profile of v2, /device:TPU:2, one launch (start us, length us, event | category | flops | bytes accessed | tf_op | source)
XLA Modules:
  0.0 51.1 jit_solution(11821693047299429849)
XLA Ops:
  0.0 49.7 %shard_map.55 = bf16[1,16,64,1024]{3,2,1,0:T(8,128)(2,1)S(1)} custom-call(bf16[2,16,64,512]{3,2,1,0:T(8,128)(2,1)} %amps.1, bf16[1,512,1024]{2,1,0:T(8,128)(2,1)} %ints.1, bf16[1,512,128]{2,1,0:T(8,128)(2,1)} %half.1, bf16[64,128]{1,0:T(8,128)(2,1)} %bitcast.2, s32[4,8,16]{2,1,0:T(8,128)} %bitcast.3), custom_call_target="tpu_custom_call" | custom-call | flops 2147483648 | bytes 6291456 | tf_op jit(solution)/shard_map/pallas_call | solution.py:335
  49.7 1.3 %copy.7 = bf16[1,16,64,1024]{3,2,1,0:T(8,128)(2,1)} copy(bf16[1,16,64,1024]{3,2,1,0:T(8,128)(2,1)S(1)} %shard_map.55) | data formatting | bytes 4194304

commit v3 on v2

--- a/solution.py
+++ b/solution.py
@@ -9,23 +9,19 @@
 TILE = 128
 CHUNK = 5
 EMPTY = 20
+LAG = 5
 SIDE = 4
 HOLD = ((0, 0), (1, 0), (0, 1), (1, 1))
 AROUND = tuple((a, b) for a in (-1, 0, 1) for b in (-1, 0, 1) if (a, b) != (0, 0))
 EDGES = (
-    (0, 1, (1, 0), (0, 2, 3)),
-    (0, 2, (0, 1), (1, 2, 3)),
-    (1, 3, (0, 1), (0, 2)),
-    (2, 3, (1, 0), (1, 3)),
-    (3, 2, (-1, 0), (0,)),
-    (3, 1, (0, -1), (1,)),
+    (0, 1, (1, 0), (0, 1, 4, 5, 6, 7)),
+    (0, 2, (0, 1), (2, 3, 4, 5, 6, 7)),
+    (1, 3, (0, 1), (0, 1, 4, 5)),
+    (2, 3, (1, 0), (2, 3, 6, 7)),
+    (3, 2, (-1, 0), (0, 1)),
+    (3, 1, (0, -1), (2, 3)),
 )
-START = (
-    (1, 1, 0), (1, 2, 1), (0, 0, 1), (0, 0, 2), (1, 1, 2), (1, 2, 2), (0, 1, 1), (0, 2, 2),
-    (1, 1, 3), (1, 2, 3),
-)
-MIDDLE = ((0, 3), (1, 3), (2, 3), (1, 2), (2, 1))
-LATE = ((3, 3), (3, 1), (3, 2))
+PIECES = tuple((CHUNK * (c // 2) + 3 * (c % 2), 3 - c % 2) for c in range(8))
 RELAYS = (
     ((1, -1), (-1, 0)), ((1, 0), (-1, 0)), ((1, 1), (-1, 0)),
     ((-1, 1), (0, -1)), ((0, 1), (0, -1)), ((1, 1), (0, -1)),
@@ -53,7 +49,7 @@
 
 def kernel(
     amps, ints, half, singles, mask_in, out,
-    lbuf, bbuf0, bbuf1, bbuf2, bbuf3, xbuf, tbuf, give, take, acc, done,
+    lbuf, bbuf0, bbuf1, bbuf2, bbuf3, xbuf, tbuf, dense, give, take, acc, done,
     mask, slot, nxt,
     lsend, lrecv, lown, inload, tsend, trecv, rsend, rrecv, dsend, drecv, bsend, brecv,
     psend, precv, osend, orecv,
@@ -129,18 +125,14 @@
         remote(block(near(-a, -b)), block(near(-a, -b)), tsend.at[k], trecv.at[k], near(a, b))
         for k, (a, b) in enumerate(AROUND)
     ]
-    t_second = [
-        remote(block(near(*what)), block(near(*what)), rsend.at[k], rrecv.at[k], near(*to))
-        for k, (what, to) in enumerate(RELAYS)
-    ]
-    t_second_from = [
-        remote(
-            block(near(what[0] - to[0], what[1] - to[1])),
-            block(near(what[0] - to[0], what[1] - to[1])),
-            rsend.at[k], rrecv.at[k], near(*to),
-        )
-        for k, (what, to) in enumerate(RELAYS)
-    ]
+    t_second, t_second_from = [], []
+    for k, ((a, b), (to_x, to_y)) in enumerate(RELAYS):
+        what = block(near(sign * a, sign * b))
+        to = near(sign * to_x, sign * to_y)
+        t_second.append(remote(what, what, rsend.at[k], rrecv.at[k], to))
+        s = sign * parity(to_x, to_y)
+        what = block(near(s * (a - to_x), s * (b - to_y)))
+        t_second_from.append(remote(what, what, rsend.at[k], rrecv.at[k], to))
 
     def holder(q, d):
         ax, ay = HOLD[q]
@@ -163,13 +155,18 @@
     for p, q, (dx, dy), chunks in EDGES:
         s = sign * parity(*HOLD[p])
         for c in chunks:
-            piece = pl.ds(c * CHUNK, CHUNK)
+            piece = pl.ds(*PIECES[c])
             b_copies[q, c] = remote(
                 bbuf[p].at[piece], bbuf[q].at[piece],
                 bsend.at[q - 1, c], brecv.at[q - 1, c], near(s * dx, s * dy),
             )
 
-    gives = [partner(give.at[q], take.at[q], psend.at[q], precv.at[q]) for q in range(4)]
+    gives = {}
+    for q in range(4):
+        for d in range(4):
+            gives[q, d] = partner(
+                give.at[q, d], take.at[q, d], psend.at[q, d], precv.at[q, d]
+            )
 
     outs = {}
     for q in range(4):
@@ -182,17 +179,6 @@
             )
 
     mask_load.wait()
-    for q in range(4):
-        j = held(q)
-
-        def count(p, c, q=q, j=j):
-            live = mask[lax.shift_right_logical(p, 3), lax.bitwise_and(p, 7), j]
-            slot[q, p] = live * (c + lax.shift_right_logical(c, 2)) + (1 - live) * EMPTY
-            return c + live
-
-        lax.fori_loop(0, 32, count, 0)
-        bbuf[q][EMPTY] = jnp.zeros((TILE, TILE), jnp.bfloat16)
-
     nxt[32] = 31
 
     def search(k, c):
@@ -216,22 +202,7 @@
 
     lax.fori_loop(0, 16, pack, 0)
 
-    own_t.wait()
-    pl.semaphore_wait(barrier, 9)
-
-    for copy in t_first:
-        copy.start()
-    for kind, one, two in START:
-        (b_copies if kind else l_copies)[one, two].start()
-    for copy in t_from:
-        copy.wait_recv()
-    for copy in t_second:
-        copy.start()
-
-    def multiply(q):
-        own_l[q].wait()
-        for d in (1, 2, 3):
-            l_copies[q, d].wait_recv()
+    def dress(q):
         j = held(q)
 
         def columns(n, carry):
@@ -242,91 +213,167 @@
                 (((1,), (1,)), ((), ())),
                 preferred_element_type=jnp.float32,
             )
-            pieces = []
             for e in range(4):
-                row = []
                 for k in range(2):
                     gate = mask[e, 2 * n + k, j].astype(jnp.float32)
                     value = bbuf[q][slot[q, 8 * e + 2 * n + k]].astype(jnp.float32)
                     value -= inner[e * TILE : (e + 1) * TILE, k * TILE : (k + 1) * TILE]
-                    row.append((gate * value).astype(jnp.bfloat16))
-                pieces.append(jnp.concatenate(row, axis=1))
-            rhs = jnp.concatenate(pieces, axis=0)
-            where = pl.ds(pl.multiple_of(n * 2 * TILE, 2 * TILE), 2 * TILE)
-            lhs = lbuf[q, other].reshape(256, 512)
-            part = jnp.dot(lhs, rhs, preferred_element_type=jnp.float32)
-            give[q, :, :, where] = part.astype(jnp.bfloat16).reshape(4, 64, 2 * TILE)
-            lhs = lbuf[q, ka].reshape(256, 512)
-            part = jnp.dot(lhs, rhs, preferred_element_type=jnp.float32)
-            acc[q, :, :, where] = part.reshape(4, 64, 2 * TILE)
+                    dense[q, n, e * TILE : (e + 1) * TILE, k * TILE : (k + 1) * TILE] = (
+                        gate * value
+                    ).astype(jnp.bfloat16)
             return carry
 
         lax.fori_loop(0, 4, columns, 0)
-        gives[q].start()
-
-    def finish(q, ds):
-        for d in ds:
-            total = acc[q, d] + take[q, d].astype(jnp.float32)
-            if d:
-                done[q, d - 1] = total.astype(jnp.bfloat16)
-            else:
-                out[0, held(q)] = total.astype(jnp.bfloat16)
-
-    def send(*which):
+
+    def multiply(q, d):
+        if d:
+            l_copies[q, d].wait_recv()
+        else:
+            own_l[q].wait()
+        lhs = jnp.concatenate([lbuf[q, other, d], lbuf[q, ka, d]], axis=0)
+        for n in range(4):
+            where = pl.ds(n * 2 * TILE, 2 * TILE)
+            part = jnp.dot(lhs, dense[q, n], preferred_element_type=jnp.float32)
+            give[q, d, :, where] = part[:64].astype(jnp.bfloat16)
+            acc[q, d, :, where] = part[64:]
+        gives[q, d].start()
+
+    def finish(q, d):
+        gives[q, d].wait_recv()
+        total = acc[q, d] + take[q, d].astype(jnp.float32)
+        if d:
+            done[q, d - 1] = total.astype(jnp.bfloat16)
+            outs[q, d].start()
+        else:
+            out[0, held(q)] = total.astype(jnp.bfloat16)
+
+    def tables():
+        for q in range(4):
+            j = held(q)
+
+            def count(p, c, q=q, j=j):
+                live = mask[lax.shift_right_logical(p, 3), lax.bitwise_and(p, 7), j]
+                slot[q, p] = live * (c + lax.shift_right_logical(c, 2)) + (1 - live) * EMPTY
+                return c + live
+
+            lax.fori_loop(0, 32, count, 0)
+            bbuf[q][EMPTY] = jnp.zeros((TILE, TILE), jnp.bfloat16)
+
+    def units(*which):
+        for k, unit in enumerate(which):
+            multiply(*unit)
+            if k >= LAG:
+                finish(*which[k - LAG])
+        for unit in which[-LAG:]:
+            finish(*unit)
+
+    def rows(*which):
         for q, d in which:
-            outs[q, d].start()
+            l_copies[q, d].start()
+
+    def blocks(q, *which):
+        for c in which:
+            b_copies[q, c].start()
+
+    def arrived(q, *which):
+        for c in which:
+            b_copies[q, c].wait_recv()
+
+    t_half = partner(tbuf.at[:, :, ka], tbuf.at[:, :, ka], dsend, drecv)
+    t_other = partner(tbuf.at[:, :, other], tbuf.at[:, :, other], dsend, drecv)
+
+    def t_on():
+        for copy in t_from:
+            copy.wait_recv()
+        for copy in t_second:
+            copy.start()
+
+    def t_across():
+        for copy in t_second_from:
+            copy.wait_recv()
+        t_half.start()
 
     def relay(q, c, r):
         b_copies[q, c].wait_recv()
         b_copies[r, c].start()
 
+    own_t.wait()
+    pl.semaphore_wait(barrier, 9)
+
+    for copy in t_first:
+        copy.start()
+    blocks(1, 0, 1)
+    blocks(2, 2, 3)
+    rows((0, 1), (0, 2))
+    blocks(1, 4, 5)
+    blocks(2, 4, 5)
+    blocks(1, 6, 7)
+    blocks(2, 6, 7)
+    rows((3, 1), (3, 2), (2, 1), (1, 2))
+    tables()
     relay(1, 0, 3)
-    relay(2, 1, 3)
-    for q, d in MIDDLE:
-        l_copies[q, d].start()
-    relay(1, 2, 3)
+    relay(2, 2, 3)
+    t_on()
+    relay(1, 1, 3)
+    relay(2, 3, 3)
     relay(3, 0, 2)
-    relay(3, 1, 1)
-    relay(2, 3, 3)
-    for q, d in LATE:
-        l_copies[q, d].start()
-
-    for copy in t_second_from:
-        copy.wait_recv()
-    t_half = partner(tbuf.at[:, :, ka], tbuf.at[:, :, ka], dsend, drecv)
-    t_half.start()
-    partner(tbuf.at[:, :, other], tbuf.at[:, :, other], dsend, drecv).wait_recv()
-
-    multiply(0)
-    gives[0].wait_recv()
-    finish(0, (0, 1, 2, 3))
-    send((0, 3), (0, 1), (0, 2))
-    for c in (1, 3):
-        b_copies[1, c].wait_recv()
-    multiply(1)
-    for c in (0, 2):
-        b_copies[2, c].wait_recv()
-    multiply(2)
-    gives[1].wait_recv()
-    finish(1, (3, 1, 2, 0))
-    gives[2].wait_recv()
-    finish(2, (3, 1, 2, 0))
-    send((1, 3), (2, 3), (1, 1), (2, 1), (1, 2), (2, 2))
-    for c in (2, 3):
-        b_copies[3, c].wait_recv()
-    multiply(3)
-    gives[3].wait_recv()
-    finish(3, (3, 1, 2, 0))
-    send((3, 3), (3, 1), (3, 2))
-
-    for copy in t_first + t_second + [t_half] + gives:
+    relay(3, 2, 1)
+    t_across()
+    relay(3, 1, 2)
+    relay(3, 3, 1)
+    relay(1, 4, 3)
+    relay(1, 5, 3)
+    relay(2, 6, 3)
+    relay(2, 7, 3)
+    rows((1, 3), (1, 1), (2, 2), (0, 3), (3, 3), (2, 3))
+    t_other.wait_recv()
+    dress(0)
+    multiply(0, 1)
+    multiply(0, 2)
+    multiply(0, 0)
+    arrived(2, 0, 1, 4, 5)
+    dress(2)
+    finish(0, 1)
+    finish(0, 2)
+    multiply(2, 1)
+    arrived(3, 4, 5, 6, 7)
+    dress(3)
+    multiply(3, 1)
+    multiply(3, 2)
+    finish(2, 1)
+    arrived(1, 2, 3, 6, 7)
+    dress(1)
+    multiply(1, 2)
+    multiply(1, 1)
+    finish(3, 1)
+    finish(3, 2)
+    multiply(1, 3)
+    multiply(1, 0)
+    multiply(2, 0)
+    finish(1, 2)
+    finish(1, 1)
+    multiply(2, 2)
+    multiply(3, 0)
+    finish(1, 3)
+    multiply(0, 3)
+    finish(2, 2)
+    multiply(3, 3)
+    multiply(2, 3)
+    finish(0, 3)
+    finish(3, 3)
+    finish(2, 3)
+    finish(0, 0)
+    finish(1, 0)
+    finish(2, 0)
+    finish(3, 0)
+
+    for copy in t_first + t_second + [t_half]:
         copy.wait_send()
-    for copies in (l_copies, b_copies, outs):
+    for copies in (l_copies, b_copies, outs, gives):
         for copy in copies.values():
             copy.wait_send()
     for copy in ins.values():
         copy.wait_recv()
-
 
 def body(lambda_amps, screened_ints, half_ints, singles, block_mask):
     bf16, f32 = jnp.bfloat16, jnp.float32
@@ -345,6 +392,7 @@
             pltpu.VMEM((EMPTY + 1, TILE, TILE), bf16),
             pltpu.VMEM((8, 4, TILE, TILE), bf16),
             pltpu.VMEM((8, 2, 2, 32, TILE), bf16),
+            pltpu.VMEM((4, 4, 512, 2 * TILE), bf16),
             pltpu.VMEM((4, 4, 64, 1024), bf16),
             pltpu.VMEM((4, 4, 64, 1024), bf16),
             pltpu.VMEM((4, 4, 64, 1024), f32),
@@ -354,8 +402,8 @@
             pltpu.SMEM((40,), jnp.int32),
             dma((4, 3)), dma((4, 3)), dma((4,)), dma((38,)),
             dma((8,)), dma((8,)), dma((7,)), dma((7,)), dma, dma,
-            dma((3, 4)), dma((3, 4)),
-            dma((4,)), dma((4,)), dma((4, 3)), dma((4, 3)),
+            dma((3, 8)), dma((3, 8)),
+            dma((4, 4)), dma((4, 4)), dma((4, 3)), dma((4, 3)),
         ],
         compiler_params=pltpu.CompilerParams(collective_id=0, has_side_effects=True),
         cost_estimate=pl.CostEstimate(

time: 51.7 us -> 46.9 us (0.907)
  Pallas kernels: 49.7 us -> 45.4 us
    pallas_call x1, Pallas kernels: 49.7 us -> 45.4 us  [body(): pl.pallas_call(kernel, out_shape=pltpu.VMEM((1, 16, 64, 1024), bf16), in_...]
where the time goes in v3:
time: 46.9 us; the launch traced here: 46.8 us
  Pallas kernels  45.4 us (97%)
  local copies, waits for them, and re-layouts  1.32 us (3%)
    pallas_call x1, Pallas kernels, body(): pl.pallas_call(kernel, out_shape=pltpu.VMEM((1, 16, 64, 1024), bf16), in_...  45.4 us
    unnamed x1, local copies, waits for them, and re-layouts  1.32 us

profile of v3, /device:TPU:2, one launch (start us, length us, event | category | flops | bytes accessed | tf_op | source)
XLA Modules:
  0.0 46.8 jit_solution(3770459691316306779)
XLA Ops:
  0.0 45.4 %shard_map.55 = bf16[1,16,64,1024]{3,2,1,0:T(8,128)(2,1)S(1)} custom-call(bf16[2,16,64,512]{3,2,1,0:T(8,128)(2,1)} %amps.1, bf16[1,512,1024]{2,1,0:T(8,128)(2,1)} %ints.1, bf16[1,512,128]{2,1,0:T(8,128)(2,1)} %half.1, bf16[64,128]{1,0:T(8,128)(2,1)} %bitcast.2, s32[4,8,16]{2,1,0:T(8,128)} %bitcast.3), custom_call_target="tpu_custom_call" | custom-call | flops 2147483648 | bytes 6291456 | tf_op jit(solution)/shard_map/pallas_call | solution.py:382
  45.4 1.3 %copy.7 = bf16[1,16,64,1024]{3,2,1,0:T(8,128)(2,1)} copy(bf16[1,16,64,1024]{3,2,1,0:T(8,128)(2,1)S(1)} %shard_map.55) | data formatting | bytes 4194304

commit v4 on v3

--- a/solution.py
+++ b/solution.py
@@ -306,9 +306,9 @@
     blocks(2, 2, 3)
     rows((0, 1), (0, 2))
     blocks(1, 4, 5)
+    blocks(2, 6, 7)
+    blocks(1, 6, 7)
     blocks(2, 4, 5)
-    blocks(1, 6, 7)
-    blocks(2, 6, 7)
     rows((3, 1), (3, 2), (2, 1), (1, 2))
     tables()
     relay(1, 0, 3)
@@ -316,15 +316,15 @@
     t_on()
     relay(1, 1, 3)
     relay(2, 3, 3)
+    relay(1, 4, 3)
+    relay(2, 6, 3)
     relay(3, 0, 2)
     relay(3, 2, 1)
+    relay(1, 5, 3)
+    relay(2, 7, 3)
     t_across()
     relay(3, 1, 2)
     relay(3, 3, 1)
-    relay(1, 4, 3)
-    relay(1, 5, 3)
-    relay(2, 6, 3)
-    relay(2, 7, 3)
     rows((1, 3), (1, 1), (2, 2), (0, 3), (3, 3), (2, 3))
     t_other.wait_recv()
     dress(0)
@@ -335,31 +335,31 @@
     dress(2)
     finish(0, 1)
     finish(0, 2)
-    multiply(2, 1)
     arrived(3, 4, 5, 6, 7)
     dress(3)
     multiply(3, 1)
     multiply(3, 2)
-    finish(2, 1)
+    multiply(2, 1)
+    multiply(2, 0)
+    multiply(3, 0)
+    finish(3, 1)
+    finish(3, 2)
     arrived(1, 2, 3, 6, 7)
     dress(1)
+    finish(2, 1)
+    multiply(1, 3)
     multiply(1, 2)
     multiply(1, 1)
-    finish(3, 1)
-    finish(3, 2)
-    multiply(1, 3)
     multiply(1, 0)
-    multiply(2, 0)
+    finish(1, 3)
     finish(1, 2)
     finish(1, 1)
+    multiply(0, 3)
     multiply(2, 2)
-    multiply(3, 0)
-    finish(1, 3)
-    multiply(0, 3)
+    multiply(3, 3)
+    finish(0, 3)
+    multiply(2, 3)
     finish(2, 2)
-    multiply(3, 3)
-    multiply(2, 3)
-    finish(0, 3)
     finish(3, 3)
     finish(2, 3)
     finish(0, 0)

time: 46.9 us -> 46.6 us (level)
  Pallas kernels: 45.4 us -> 44.9 us
    pallas_call x1, Pallas kernels: 45.4 us -> 44.9 us  [body(): pl.pallas_call(kernel, out_shape=pltpu.VMEM((1, 16, 64, 1024), bf16), in_...]
where the time goes in v4:
time: 46.6 us; the launch traced here: 46.3 us
  Pallas kernels  44.9 us (96%)
  local copies, waits for them, and re-layouts  1.32 us (3%)
    pallas_call x1, Pallas kernels, body(): pl.pallas_call(kernel, out_shape=pltpu.VMEM((1, 16, 64, 1024), bf16), in_...  44.9 us
    unnamed x1, local copies, waits for them, and re-layouts  1.32 us

profile of v4, /device:TPU:2, one launch (start us, length us, event | category | flops | bytes accessed | tf_op | source)
XLA Modules:
  0.0 46.3 jit_solution(10011559732174487874)
XLA Ops:
  0.0 44.9 %shard_map.55 = bf16[1,16,64,1024]{3,2,1,0:T(8,128)(2,1)S(1)} custom-call(bf16[2,16,64,512]{3,2,1,0:T(8,128)(2,1)} %amps.1, bf16[1,512,1024]{2,1,0:T(8,128)(2,1)} %ints.1, bf16[1,512,128]{2,1,0:T(8,128)(2,1)} %half.1, bf16[64,128]{1,0:T(8,128)(2,1)} %bitcast.2, s32[4,8,16]{2,1,0:T(8,128)} %bitcast.3), custom_call_target="tpu_custom_call" | custom-call | flops 2147483648 | bytes 6291456 | tf_op jit(solution)/shard_map/pallas_call | solution.py:382
  44.9 1.3 %copy.7 = bf16[1,16,64,1024]{3,2,1,0:T(8,128)(2,1)} copy(bf16[1,16,64,1024]{3,2,1,0:T(8,128)(2,1)S(1)} %shard_map.55) | data formatting | bytes 4194304

commit v5 on v4

--- a/solution.py
+++ b/solution.py
@@ -331,10 +331,10 @@
     multiply(0, 1)
     multiply(0, 2)
     multiply(0, 0)
+    finish(0, 1)
+    finish(0, 2)
     arrived(2, 0, 1, 4, 5)
     dress(2)
-    finish(0, 1)
-    finish(0, 2)
     arrived(3, 4, 5, 6, 7)
     dress(3)
     multiply(3, 1)

time: 46.6 us -> 46.7 us (level)
  no operation moved by 1% of the time
where the time goes in v5:
time: 46.7 us; the launch traced here: 46.3 us
  Pallas kernels  44.9 us (96%)
  local copies, waits for them, and re-layouts  1.32 us (3%)
    pallas_call x1, Pallas kernels, body(): pl.pallas_call(kernel, out_shape=pltpu.VMEM((1, 16, 64, 1024), bf16), in_...  44.9 us
    unnamed x1, local copies, waits for them, and re-layouts  1.32 us

profile of v5, /device:TPU:2, one launch (start us, length us, event | category | flops | bytes accessed | tf_op | source)
XLA Modules:
  0.0 46.3 jit_solution(1294338989344406999)
XLA Ops:
  0.0 44.9 %shard_map.55 = bf16[1,16,64,1024]{3,2,1,0:T(8,128)(2,1)S(1)} custom-call(bf16[2,16,64,512]{3,2,1,0:T(8,128)(2,1)} %amps.1, bf16[1,512,1024]{2,1,0:T(8,128)(2,1)} %ints.1, bf16[1,512,128]{2,1,0:T(8,128)(2,1)} %half.1, bf16[64,128]{1,0:T(8,128)(2,1)} %bitcast.2, s32[4,8,16]{2,1,0:T(8,128)} %bitcast.3), custom_call_target="tpu_custom_call" | custom-call | flops 2147483648 | bytes 6291456 | tf_op jit(solution)/shard_map/pallas_call | solution.py:382
  44.9 1.3 %copy.7 = bf16[1,16,64,1024]{3,2,1,0:T(8,128)(2,1)} copy(bf16[1,16,64,1024]{3,2,1,0:T(8,128)(2,1)S(1)} %shard_map.55) | data formatting | bytes 4194304

commit v6 on v4

--- a/solution.py
+++ b/solution.py
@@ -322,10 +322,10 @@
     relay(3, 2, 1)
     relay(1, 5, 3)
     relay(2, 7, 3)
-    t_across()
     relay(3, 1, 2)
     relay(3, 3, 1)
     rows((1, 3), (1, 1), (2, 2), (0, 3), (3, 3), (2, 3))
+    t_across()
     t_other.wait_recv()
     dress(0)
     multiply(0, 1)

time: 46.6 us -> 46.6 us (level)
  no operation moved by 1% of the time
where the time goes in v6:
time: 46.6 us; the launch traced here: 46.3 us
  Pallas kernels  44.9 us (96%)
  local copies, waits for them, and re-layouts  1.32 us (3%)
    pallas_call x1, Pallas kernels, body(): pl.pallas_call(kernel, out_shape=pltpu.VMEM((1, 16, 64, 1024), bf16), in_...  44.9 us
    unnamed x1, local copies, waits for them, and re-layouts  1.32 us

profile of v6, /device:TPU:2, one launch (start us, length us, event | category | flops | bytes accessed | tf_op | source)
XLA Modules:
  0.0 46.3 jit_solution(8684981779401332119)
XLA Ops:
  0.0 44.9 %shard_map.55 = bf16[1,16,64,1024]{3,2,1,0:T(8,128)(2,1)S(1)} custom-call(bf16[2,16,64,512]{3,2,1,0:T(8,128)(2,1)} %amps.1, bf16[1,512,1024]{2,1,0:T(8,128)(2,1)} %ints.1, bf16[1,512,128]{2,1,0:T(8,128)(2,1)} %half.1, bf16[64,128]{1,0:T(8,128)(2,1)} %bitcast.2, s32[4,8,16]{2,1,0:T(8,128)} %bitcast.3), custom_call_target="tpu_custom_call" | custom-call | flops 2147483648 | bytes 6291456 | tf_op jit(solution)/shard_map/pallas_call | solution.py:382
  44.9 1.3 %copy.7 = bf16[1,16,64,1024]{3,2,1,0:T(8,128)(2,1)} copy(bf16[1,16,64,1024]{3,2,1,0:T(8,128)(2,1)S(1)} %shard_map.55) | data formatting | bytes 4194304
